TPU v7x, 32 devices: a whole 2x2x4 slice. The times are simulated.
32 devices in a mesh: groups: 2 (over y), space: 4 (over z), mp: 2 (over x), sub: 2 (over core).
Axes of the slice: x: 2, y: 2, z: 4, core: 2. Of those that a mesh axis runs over, the one named last changes fastest.
Arguments:
- voxels: bfloat16 [24576, 512], P(('groups', 'space', 'sub')), parts along dimension 0, may hold values from -6 to 6
- window_ids: int32 [24576], P(('groups', 'space', 'sub')), parts along dimension 0, may hold values from 0 to 127, as said below
- voxel_slots: int32 [24576], P(('groups', 'space', 'sub')), parts along dimension 0, may hold values from 0 to 255, as said below
- window_counts: int32 [256], P('groups'), parts along dimension 0, may hold values from 0 to 256, as said below
- norm_gain: float32 [512], replicated, may hold values from 0.25 to 1.75
- w_query_key: bfloat16 [2, 512, 512], P(None, None, 'mp'), may hold values from -2 to 2
- w_value: bfloat16 [512, 512], P(None, 'mp'), may hold values from -0.25 to 0.25
- w_out: bfloat16 [512, 512], P('mp'), may hold values from -0.25 to 0.25
- ffn_gain: float32 [512], replicated, may hold values from 0.25 to 1.75
- w_up: bfloat16 [512, 2048], P(None, 'mp'), may hold values from -0.25 to 0.25
- w_down: bfloat16 [2048, 512], P('mp'), may hold values from -0.125 to 0.125
Outputs:
- result: bfloat16 [24576, 512], P(('groups', 'space', 'sub'), 'mp'), parts along dimension 0
There are 2 independent parts, one for each index of `groups`. A program takes and returns all parts, laid end to end along the dimension named above; an argument that names none is the same for every part. Nothing has to cross between parts.
Inputs may be any that keep to these rules, and one draw needn't show every extreme that they name: `window_ids`: window w belongs to owner w // 16 (its index along space+sub) as that owner's window w % 16. On the voxels of one device at most 384 lie in windows of one owner, and in every draw some owner has exactly 384 voxels of every device. `voxel_slots`: the voxels of a window hold slots 0 to its count - 1, each once. window_counts[w] is the number of voxels with window id w; some window holds 256.
All inputs are finite; a program needn't handle non-finite values.
Results may differ from a plain program's by a relative error of at most 0.012.
Values may be sent and summed in bfloat16 or wider, within the bound.
A program may use at most 128 MiB of HBM per device.

v0:
```python
import functools
import math

import jax
import jax.numpy as jnp
from jax import lax
from jax.experimental import pallas as pl
from jax.experimental.pallas import tpu as pltpu
from jax.sharding import PartitionSpec as P

HDIM = 64
WLEN = 256
WIN_DEV = 16
BASE = 64
MESH = pl.DeviceIdType.MESH
VMEM = pl.BlockSpec(memory_space=pltpu.VMEM)
f32 = jnp.float32
bf16 = jnp.bfloat16


def normalize(values_in, gain):
    row_mean = jnp.mean(values_in, axis=-1, keepdims=True)
    centred = values_in - row_mean
    variance = jnp.mean(centred * centred, axis=-1, keepdims=True)
    return centred * lax.rsqrt(variance + 1e-05) * gain


def iota(shape, dim):
    return lax.broadcasted_iota(jnp.int32, shape, dim)


def one_hot(found):
    return jnp.where(found, f32(1), f32(0)).astype(bf16)


def dot(a, b, dims=((1,), (0,))):
    return lax.dot_general(a, b, (dims, ((), ())), preferred_element_type=f32)


def greet(owners, subs, mp_n, me, m):
    barrier = pltpu.get_barrier_semaphore()
    for k in range(1, owners):
        t = (me + k) % owners
        pl.semaphore_signal(
            barrier, inc=1, device_id={"space": t // subs, "sub": t % subs}, device_id_type=MESH
        )
    for p in range(1, mp_n):
        pl.semaphore_signal(
            barrier, inc=1, device_id={"mp": (m + p) % mp_n}, device_id_type=MESH
        )
    pl.semaphore_wait(barrier, owners - 1 + mp_n - 1)


def to_owner(src, dst, sems, slot, target, subs):
    return pltpu.make_async_remote_copy(
        src_ref=src,
        dst_ref=dst,
        send_sem=sems[0].at[slot],
        recv_sem=sems[1].at[slot],
        device_id={"space": target // subs, "sub": target % subs},
        device_id_type=MESH,
    )


def to_mp(src, dst, sems, index, peer):
    return pltpu.make_async_remote_copy(
        src_ref=src,
        dst_ref=dst,
        send_sem=sems[0].at[index],
        recv_sem=sems[1].at[index],
        device_id={"mp": peer},
        device_id_type=MESH,
    )


def dispatch_kernel(
    spaces, subs, mp_n, normed, index, digits, out_rows, padded, spots, whole_out,
    outbuf, nearbuf, arrived, spotbuf, ms, mr, ps, pr, ss, sr, ws, wr,
):
    owners = spaces * subs
    far = owners - subs
    sp, sb, m = lax.axis_index("space"), lax.axis_index("sub"), lax.axis_index("mp")
    me = sp * subs + sb
    cap, part, rows = outbuf.shape[1], outbuf.shape[2], normed.shape[0]
    greet(owners, subs, mp_n, me, m)
    for p in range(1, mp_n):
        to_mp(out_rows, whole_out.at[m], (ws, wr), p - 1, (m + p) % mp_n).start()
    whole_out[m] = out_rows[...]

    def sink(slot):
        return (sp + slot // subs + 1) % spaces * subs + (sb + slot % subs) % subs

    def source(slot):
        return (sp + spaces - slot // subs - 1) % spaces * subs + (sb + subs - slot % subs) % subs

    def find(slot, t):
        hit = one_hot(index[...] == iota((cap, rows), 0) + t * cap)
        parts = dot(digits[...], hit, ((1,), (1,)))
        place = parts[0:1] * BASE + parts[1:2] + (1 - parts[2:3]) * (WIN_DEV * WLEN)
        spotbuf[slot] = place.astype(jnp.int32)
        return hit

    def spot_copy(slot, s, t):
        return to_owner(spotbuf.at[slot], spots.at[s], (ps, pr), slot, t, subs)

    def far_copy(slot, s, t):
        return to_owner(outbuf.at[slot], arrived.at[s, m], (ms, mr), slot, t, subs)

    def near_copy(j, s, t):
        return to_owner(nearbuf.at[j], arrived.at[s], (ms, mr), far + j, t, subs)

    def side_copy(slot, p, half, s):
        return to_mp(
            arrived.at[s, m], arrived.at[s, half], (ss, sr), slot * (mp_n - 1) + p - 1,
            (m + p) % mp_n,
        )

    def send(slot):
        far_copy(slot, me, sink(slot)).start()
        spot_copy(slot, me, sink(slot)).start()

    def build(slot, carry):
        hit = find(slot, sink(slot))
        mine = normed[:, pl.ds(pl.multiple_of(m * part, part), part)]
        outbuf[slot] = dot(hit, mine).astype(bf16)

        @pl.when(slot > 0)
        def _():
            send(slot - 1)

        return carry

    lax.fori_loop(0, far, build, 0)
    for j in range(subs):
        hit = find(far + j, sp * subs + (sb + j) % subs)
        for h in range(mp_n):
            nearbuf[j, h] = dot(hit, normed[:, h * part : (h + 1) * part]).astype(bf16)
        if j == 0:
            send(far - 1)
        elif j > 1:
            near_copy(j - 1, me, sp * subs + (sb + j - 1) % subs).start()
            spot_copy(far + j - 1, me, sp * subs + (sb + j - 1) % subs).start()
    spots[me] = spotbuf[far]
    chunk = 4 * WLEN

    def put(s, blocks, first):
        row = spots[s]

        def span(c, carry):
            hit = one_hot(row == iota((chunk, cap), 0) + c * chunk)
            here = pl.ds(c * chunk, chunk)
            for h in range(mp_n):
                new = dot(hit, blocks[h]).astype(bf16)
                if not first:
                    new += padded[here, h * part : (h + 1) * part]
                padded[here, h * part : (h + 1) * part] = new
            return carry

        lax.fori_loop(0, padded.shape[0] // chunk, span, 0)

    put(me, nearbuf.at[0], True)
    for j in range(max(subs - 1, 1), subs):
        near_copy(j, me, sp * subs + (sb + j) % subs).start()
        spot_copy(far + j, me, sp * subs + (sb + j) % subs).start()

    def settle(slot):
        s = source(slot)
        for p in range(1, mp_n):
            side_copy(slot, p, (m + mp_n - p) % mp_n, s).wait()
        spot_copy(slot, s, s).wait()
        put(s, arrived.at[s], False)

    def onward(slot, carry):
        s = source(slot)
        far_copy(slot, s, s).wait()
        for p in range(1, mp_n):
            side_copy(slot, p, m, s).start()

        @pl.when(slot > 0)
        def _():
            settle(slot - 1)

        return carry

    lax.fori_loop(0, far, onward, 0)
    for j in range(1, subs):
        s = sp * subs + (sb + subs - j) % subs
        near_copy(j, s, s).wait()
        spot_copy(far + j, s, s).wait()
        put(s, arrived.at[s], False)
    settle(far - 1)
    for p in range(1, mp_n):
        to_mp(
            out_rows, whole_out.at[(m + mp_n - p) % mp_n], (ws, wr), p - 1, (m + p) % mp_n
        ).wait()


def dispatch(spaces, subs, mp_n, cap, normed, index, digits, out_rows):
    owners = spaces * subs
    width = normed.shape[1]
    part = width // mp_n
    dma = pltpu.SemaphoreType.DMA
    side = owners * (mp_n - 1)
    return pl.pallas_call(
        functools.partial(dispatch_kernel, spaces, subs, mp_n),
        out_shape=(
            jax.ShapeDtypeStruct((WIN_DEV * WLEN, width), bf16),
            jax.ShapeDtypeStruct((owners, 1, cap), jnp.int32),
            jax.ShapeDtypeStruct((mp_n,) + out_rows.shape, bf16),
        ),
        in_specs=[VMEM] * 4,
        out_specs=(VMEM, VMEM, VMEM),
        scratch_shapes=[
            pltpu.VMEM((owners - subs, cap, part), bf16),
            pltpu.VMEM((subs, mp_n, cap, part), bf16),
            pltpu.VMEM((owners, mp_n, cap, part), bf16),
            pltpu.VMEM((owners, 1, cap), jnp.int32),
            dma((owners,)), dma((owners,)), dma((owners,)), dma((owners,)),
            dma((side,)), dma((side,)), dma((mp_n,)), dma((mp_n,)),
        ],
        compiler_params=pltpu.CompilerParams(collective_id=0, has_side_effects=True),
        name="dispatch",
    )(normed, index, digits, out_rows)


def attend_kernel(group, counts, padded, w_qk, w_v, mixture):
    step = pl.program_id(0)
    local = w_v.shape[1]
    heads = local // HDIM
    rows_in = padded[...]
    queries = dot(rows_in, w_qk[0]).astype(bf16)
    keys = dot(rows_in, w_qk[1]).astype(bf16)
    values = dot(rows_in, w_v[...]).astype(bf16)
    head_of = iota((1, local), 1) // HDIM
    masks = [jnp.where(head_of == h, f32(1), f32(0)).astype(bf16) for h in range(heads)]
    for g in range(group):
        span = slice(g * WLEN, (g + 1) * WLEN)
        q, k, v = queries[span], keys[span], values[span]
        stacked = jnp.concatenate([q * masks[h] for h in range(heads)], axis=0)
        scores = dot(stacked, k, ((1,), (1,))) * f32(HDIM ** -0.5)
        live = iota((1, WLEN), 1) < counts[step * group + g]
        scores = jnp.where(live, scores, f32(-1e30))
        weights = jnp.exp(scores - jnp.max(scores, axis=-1, keepdims=True))
        scale = 1.0 / jnp.sum(weights, axis=-1, keepdims=True)
        mixed = dot((weights * scale).astype(bf16), v)
        out = mixed[:WLEN]
        for h in range(1, heads):
            out = jnp.where(head_of == h, mixed[h * WLEN : (h + 1) * WLEN], out)
        mixture[span, :] = out.astype(bf16)


def attend(counts, padded, w_qk, w_v, group=2):
    local = w_v.shape[1]
    slots = group * WLEN
    whole = lambda a: pl.BlockSpec(a.shape, lambda i: (0,) * a.ndim)
    return pl.pallas_call(
        functools.partial(attend_kernel, group),
        grid=(WIN_DEV // group,),
        out_shape=jax.ShapeDtypeStruct((WIN_DEV * WLEN, local), bf16),
        in_specs=[
            pl.BlockSpec(memory_space=pltpu.SMEM),
            pl.BlockSpec((slots, padded.shape[1]), lambda i: (i, 0)),
            whole(w_qk),
            whole(w_v),
        ],
        out_specs=pl.BlockSpec((slots, local), lambda i: (i, 0)),
        name="attend",
    )(counts, padded, w_qk, w_v)


def answer_kernel(
    owners, subs, mp_n, mixture, column, index, attended, outbuf, answers, total, ms, mr, ss, sr
):
    me = lax.axis_index("space") * subs + lax.axis_index("sub")
    m = lax.axis_index("mp")
    cap, local = outbuf.shape[1], outbuf.shape[2]
    rows = index.shape[0]
    span = 4 * WLEN
    greet(owners, subs, mp_n, me, m)

    def main_copy(slot, s, t):
        return to_owner(outbuf.at[slot], answers.at[m, s], (ms, mr), slot, t, subs)

    def side_copy(slot, p, src, half, s):
        return to_mp(
            src, answers.at[half, s], (ss, sr), slot * (mp_n - 1) + p - 1, (m + p) % mp_n
        )

    def send(slot):
        t = (me + slot) % owners

        @pl.when(slot > 0)
        def _():
            main_copy(slot, me, t).start()

        @pl.when(slot == 0)
        def _():
            for p in range(1, mp_n):
                side_copy(0, p, outbuf.at[0], m, me).start()

    def onward(slot, carry):
        s = (me + owners - slot) % owners
        main_copy(slot, s, s).wait()
        for p in range(1, mp_n):
            side_copy(slot, p, answers.at[m, s], m, s).start()
        return carry

    def build(slot, carry):
        place = column[(me + slot) % owners]
        total[...] = jnp.zeros_like(total)

        def add(c, inner):
            hit = one_hot(place == iota((cap, span), 1) + c * span)
            total[...] += dot(hit, mixture[pl.ds(c * span, span), :])
            return inner

        lax.fori_loop(0, mixture.shape[0] // span, add, 0)
        outbuf[slot] = total[...].astype(bf16)

        @pl.when(slot > 0)
        def _():
            send(slot - 1)

        @pl.when((slot >= 4) & (slot % 2 == 0))
        def _():
            onward(slot // 2 - 1, 0)

        return carry

    lax.fori_loop(0, owners, build, 0)
    send(owners - 1)
    answers[m, me] = outbuf[0]
    attended[...] = jnp.zeros_like(attended)

    def settle(slot):
        s = (me + owners - slot) % owners
        for p in range(1, mp_n):
            side_copy(slot, p, outbuf.at[slot], (m + mp_n - p) % mp_n, s).wait()
        hit = one_hot(index[...] == iota((rows, cap), 1) + s * cap)
        for h in range(mp_n):
            attended[h] += dot(hit, answers[h, s]).astype(bf16)

    ahead = max((owners - 1) // 2 - 1, 0)

    def drain(slot, carry):
        onward(slot, 0)
        settle(slot - ahead - 1)
        return carry

    lax.fori_loop(ahead + 1, owners, drain, 0)

    def rest(slot, carry):
        settle(slot)
        return carry

    lax.fori_loop(owners - ahead - 1, owners, rest, 0)


def answer(owners, subs, mp_n, cap, mixture, column, index):
    local = mixture.shape[1]
    dma = pltpu.SemaphoreType.DMA
    side = owners * (mp_n - 1)
    return pl.pallas_call(
        functools.partial(answer_kernel, owners, subs, mp_n),
        out_shape=jax.ShapeDtypeStruct((mp_n, index.shape[0], local), bf16),
        in_specs=[VMEM] * 3,
        out_specs=VMEM,
        scratch_shapes=[
            pltpu.VMEM((owners, cap, local), bf16),
            pltpu.VMEM((mp_n, owners, cap, local), bf16),
            pltpu.VMEM((cap, local), f32),
            dma((owners,)), dma((owners,)), dma((side,)), dma((side,)),
        ],
        compiler_params=pltpu.CompilerParams(collective_id=1, has_side_effects=True),
        name="answer",
    )(mixture, column, index)


def pick(value, which, pieces):
    part = value.shape[1] // pieces
    out = value[:, :part]
    for j in range(1, pieces):
        out = jnp.where(which == j, value[:, j * part : (j + 1) * part], out)
    return out


def ffn_kernel(
    mp_n, block, voxels, attended, w_out, gain, w_up, w_down, result,
    sendbuf, recvbuf, mine, ss, sr,
):
    m = lax.axis_index("mp")
    rows = voxels.shape[0]
    steps = rows // block
    barrier = pltpu.get_barrier_semaphore()
    for p in range(1, mp_n):
        pl.semaphore_signal(
            barrier, inc=1, device_id={"mp": (m + p) % mp_n}, device_id_type=MESH
        )
    pl.semaphore_wait(barrier, mp_n - 1)

    def copy(b, p):
        span = pl.ds(b * block, block)
        return to_mp(
            sendbuf.at[p - 1, span], recvbuf.at[p - 1, span], (ss, sr),
            b * (mp_n - 1) + p - 1, (m + p) % mp_n,
        )

    def work(b, carry):
        span = pl.ds(b * block, block)
        after = voxels[span, :].astype(f32)
        for h in range(mp_n):
            after += dot(attended[h, span, :], w_out[h])
        normed = normalize(after, gain[...]).astype(bf16)
        hidden = jax.nn.gelu(dot(normed, w_up[...]), approximate=True).astype(bf16)
        terms = dot(hidden, w_down[...])
        mine[span, :] = pick(after, m, mp_n) + pick(terms, m, mp_n)
        for p in range(1, mp_n):
            sendbuf[p - 1, span, :] = pick(terms, (m + p) % mp_n, mp_n).astype(bf16)

        @pl.when(b > 0)
        def _():
            for p in range(1, mp_n):
                copy(b - 1, p).start()

        return carry

    lax.fori_loop(0, steps, work, 0)
    for p in range(1, mp_n):
        copy(steps - 1, p).start()

    def finish(b, carry):
        span = pl.ds(b * block, block)
        out = mine[span, :]
        for p in range(1, mp_n):
            copy(b, p).wait()
            out += recvbuf[p - 1, span, :].astype(f32)
        result[span, :] = out.astype(bf16)
        return carry

    lax.fori_loop(0, steps, finish, 0)


def ffn(mp_n, voxels, attended, w_out, gain, w_up, w_down):
    rows, width = voxels.shape
    part = width // mp_n
    block = math.gcd(rows, 256)
    dma = pltpu.SemaphoreType.DMA
    side = rows // block * (mp_n - 1)
    return pl.pallas_call(
        functools.partial(ffn_kernel, mp_n, block),
        out_shape=jax.ShapeDtypeStruct((rows, part), bf16),
        in_specs=[VMEM] * 6,
        out_specs=VMEM,
        scratch_shapes=[
            pltpu.VMEM((mp_n - 1, rows, part), bf16),
            pltpu.VMEM((mp_n - 1, rows, part), bf16),
            pltpu.VMEM((rows, part), f32),
            dma((side,)), dma((side,)),
        ],
        compiler_params=pltpu.CompilerParams(collective_id=2, has_side_effects=True),
        name="ffn",
    )(voxels, attended, w_out, gain, w_up, w_down)


def shards(
    subs,
    voxels,
    window_ids,
    voxel_slots,
    window_counts,
    norm_gain,
    w_query_key,
    w_value,
    w_out,
    ffn_gain,
    w_up,
    w_down,
):
    owners = lax.axis_size(("space", "sub"))
    my_index = lax.axis_index(("space", "sub"))
    mp_n = lax.axis_size("mp")
    rows = voxels.shape[0]
    cap = 2 * rows // owners
    normed = normalize(voxels.astype(f32), norm_gain).astype(bf16)
    destination = window_ids // WIN_DEV
    position = window_ids % WIN_DEV * WLEN + voxel_slots
    target = (jnp.arange(owners, dtype=jnp.int32)[:, None] == destination[None, :]).astype(
        jnp.int32
    )
    before = jnp.sum((jnp.cumsum(target, axis=1) - target) * target, axis=0)
    send_index = destination * cap + before
    digits = jnp.stack(
        [position // BASE, position % BASE, jnp.ones_like(position)]
        + [jnp.zeros_like(position)] * 5
    ).astype(bf16)
    padded, spots, whole_out = dispatch(
        owners // subs, subs, mp_n, cap, normed, send_index[None, :], digits, w_out
    )
    counts = lax.dynamic_slice_in_dim(window_counts, my_index * WIN_DEV, WIN_DEV, 0)
    mixture = attend(counts, padded, w_query_key, w_value)
    attended = answer(
        owners, subs, mp_n, cap, mixture, spots.reshape(owners, cap, 1), send_index[:, None]
    )
    return ffn(mp_n, voxels, attended, whole_out, ffn_gain[None, :], w_up, w_down)


def solution(mesh):
    return jax.shard_map(
        functools.partial(shards, mesh.shape["sub"]),
        mesh=mesh,
        in_specs=(
            P(("groups", "space", "sub"), None),
            P(("groups", "space", "sub")),
            P(("groups", "space", "sub")),
            P("groups"),
            P(),
            P(None, None, "mp"),
            P(None, "mp"),
            P("mp", None),
            P(),
            P(None, "mp"),
            P("mp", None),
        ),
        out_specs=P(("groups", "space", "sub"), "mp"),
        check_vma=False,
    )
```

profile of v0, /device:TPU:12, one launch (start us, length us, event | category | flops | bytes accessed | tf_op | source)
XLA Modules:
  0.0 182.9 jit_solution(1475353360346023475)
XLA Ops:
  0.0 0.0 copy-start
  0.0 0.0 copy-start.2
  0.0 0.9 fusion.9
  0.9 2.3 %reduce-window.6 = s32[8,12,128]{2,1,0:T(8,128)S(1)} reduce-window(s32[8,12,128]{2,1,0:T(8,128)S(1)} %fusion.5, s32[]{:T(128)} %constant.69.clone.1), window={size=1x1x128 pad=0_0x0_0x127_0}, to_apply=%region_2.3 | reduce-window | flops 1560576 | bytes 98308 | tf_op jit(solution)/shard_map/reduce-window
  3.2 0.3 slice_reduce_fusion
  3.4 0.2 reduce-window.9
  3.6 0.1 select_reduce_fusion
  3.7 0.7 bitcast_add_fusion
  4.4 0.6 broadcast_in_dim.6.index
  5.1 0.7 stack.18.digits
  5.8 1.7 convert_reduce_fusion
  7.5 0.0 copy-done
  7.5 0.0 copy-start.3
  7.5 0.8 fusion.2
  8.3 0.0 copy-done.2
  8.3 1.8 fusion.4.normed
  10.1 62.5 %dispatch.1 = (bf16[4096,512]{1,0:T(8,128)(2,1)}, s32[8,1,384]{2,1,0:T(1,128)}, bf16[2,256,512]{2,1,0:T(8,128)(2,1)}) custom-call(bf16[1536,512]{1,0:T(8,128)(2,1)} %fusion.4.normed, s32[1,1536]{1,0:T(1,128)} %broadcast_in_dim.6.index, bf16[8,1536]{1,0:T(8,128)(2,1)} %stack.18.digits, bf16[256,512]{1,0:T(8,128)(2,1)} %out_rows.1), custom_call_target="tpu_custom_call" | custom-call | tf_op jit(solution)/shard_map/dispatch/pallas_call | solution.py:204
  72.6 0.0 copy-done.3
  72.6 0.6 dynamic_slice.3.counts
  73.2 0.0 copy-start.1
  73.2 17.0 %attend.1.mixture = bf16[4096,256]{1,0:T(8,128)(2,1)} custom-call(s32[16]{0:T(128)} %dynamic_slice.3.counts, bf16[4096,512]{1,0:T(8,128)(2,1)} %get-tuple-element.8.padded, bf16[2,512,256]{2,1,0:T(8,128)(2,1)} %w_qk.1, bf16[512,256]{1,0:T(8,128)(2,1)} %w_v.1), custom_call_target="tpu_custom_call" | custom-call | tf_op jit(solution)/shard_map/attend/pallas_call | solution.py:256
  90.2 0.0 copy-done.1
  90.2 1.5 reshape.43.column
  91.7 1.1 broadcast_in_dim.17.index
  92.8 63.0 %answer.1.attended = bf16[2,1536,256]{2,1,0:T(8,128)(2,1)} custom-call(bf16[4096,256]{1,0:T(8,128)(2,1)} %attend.1.mixture, s32[8,384,1]{2,1,0:T(8,128)} %reshape.43.column, s32[1536,1]{1,0:T(8,128)} %broadcast_in_dim.17.index), custom_call_target="tpu_custom_call" | custom-call | tf_op jit(solution)/shard_map/answer/pallas_call | solution.py:363
  155.9 25.0 %ffn.1 = bf16[1536,256]{1,0:T(8,128)(2,1)} custom-call(bf16[1536,512]{1,0:T(8,128)(2,1)} %voxels.1, bf16[2,1536,256]{2,1,0:T(8,128)(2,1)} %answer.1.attended, bf16[2,256,512]{2,1,0:T(8,128)(2,1)} %get-tuple-element.10.w_out, f32[1,512]{1,0:T(1,128)} %bitcast.7, bf16[512,1024]{1,0:T(8,128)(2,1)} %w_up.1, bf16[1024,512]{1,0:T(8,128)(2,1)} %w_down.1), custom_call_target="tpu_custom_call" | custom-call | tf_op jit(solution)/shard_map/ffn/pallas_call | solution.py:449
  180.9 2.1 %copy.15 = bf16[1536,256]{1,0:T(8,128)(2,1)} copy(bf16[1536,256]{1,0:T(8,128)(2,1)} %ffn.1) | data formatting | bytes 1572864
  (10 shorter events, 0.1 us)
Async XLA Ops:
  0.0 7.5 %copy-start = (bf16[1536,512]{1,0:T(8,128)(2,1)S(1)}, bf16[1536,512]{1,0:T(8,128)(2,1)}, u32[]{:S(2)}) copy-start(bf16[1536,512]{1,0:T(8,128)(2,1)} %voxels.1) | copy-start | bytes 4718596
  0.0 8.3 %copy-start.2 = (f32[512]{0:T(512)S(1)}, f32[512]{0:T(512)}, u32[]{:S(2)}) copy-start(f32[512]{0:T(512)} %param.15) | copy-start | bytes 6148
  7.5 65.1 %copy-start.3 = (s32[128]{0:T(128)S(1)}, s32[128]{0:T(128)}, u32[]{:S(2)}) copy-start(s32[128]{0:T(128)} %param.14) | copy-start | bytes 1540
  73.2 17.0 %copy-start.1 = (s32[8,1,384]{2,1,0:T(1,128)S(1)}, s32[8,1,384]{2,1,0:T(1,128)}, u32[]{:S(2)}) copy-start(s32[8,1,384]{2,1,0:T(1,128)} %get-tuple-element.9) | copy-start | bytes 36868
where the time goes:
time: 184 us; the launch traced here: 183 us
  Pallas kernels  168 us (91%)
  other arithmetic  8.4 us (5%)
  local copies, waits for them, and re-layouts  6.86 us (4%)
    pallas_call x1, Pallas kernels, answer(): pl.pallas_call(functools.partial(answer_kernel, owners, subs, mp_n), out_...  63 us
    pallas_call x1, Pallas kernels, dispatch(): pl.pallas_call(functools.partial(dispatch_kernel, spaces, subs, mp_n), ou...  62.5 us
    pallas_call x1, Pallas kernels, ffn(): pl.pallas_call(functools.partial(ffn_kernel, mp_n, block), out_shape=jax....  25 us
    pallas_call x1, Pallas kernels, attend(): pl.pallas_call(functools.partial(attend_kernel, group), grid=(WIN_DEV //...  17 us

commit v1 on v0

v1 whole, which is shorter than its diff:
```python
import functools
import math

import jax
import jax.numpy as jnp
from jax import lax
from jax.experimental import pallas as pl
from jax.experimental.pallas import tpu as pltpu
from jax.sharding import PartitionSpec as P

HDIM = 64
WLEN = 256
WIN_DEV = 16
BASE = 64
SLOTS = WIN_DEV * WLEN
MESH = pl.DeviceIdType.MESH
VMEM = pl.BlockSpec(memory_space=pltpu.VMEM)
SMEM = pl.BlockSpec(memory_space=pltpu.SMEM)
ANY = pl.BlockSpec(memory_space=pl.ANY)
f32 = jnp.float32
bf16 = jnp.bfloat16


def normalize(values_in, gain):
    row_mean = jnp.mean(values_in, axis=-1, keepdims=True)
    centred = values_in - row_mean
    variance = jnp.mean(centred * centred, axis=-1, keepdims=True)
    return centred * lax.rsqrt(variance + 1e-05) * gain


def iota(shape, dim):
    return lax.broadcasted_iota(jnp.int32, shape, dim)


def one_hot(found):
    return jnp.where(found, f32(1), f32(0)).astype(bf16)


def dot(a, b, dims=((1,), (0,))):
    return lax.dot_general(a, b, (dims, ((), ())), preferred_element_type=f32)


def greet(owners, subs, mp_n, me, m):
    barrier = pltpu.get_barrier_semaphore()
    for k in range(1, owners):
        t = (me + k) % owners
        pl.semaphore_signal(
            barrier, inc=1, device_id={"space": t // subs, "sub": t % subs}, device_id_type=MESH
        )
    for p in range(1, mp_n):
        pl.semaphore_signal(
            barrier, inc=1, device_id={"mp": (m + p) % mp_n}, device_id_type=MESH
        )
    return lambda: pl.semaphore_wait(barrier, owners - 1 + mp_n - 1)


def remote(src, dst, sems, index, device):
    return pltpu.make_async_remote_copy(
        src_ref=src,
        dst_ref=dst,
        send_sem=sems[0].at[index],
        recv_sem=sems[1].at[index],
        device_id=device,
        device_id_type=MESH,
    )


def column_of(row):
    return jnp.transpose(jnp.broadcast_to(row, (128, row.shape[1])))


def widen(column, width):
    return jnp.concatenate([column] * (width // 128), axis=1)


def block_kernel(
    spaces, subs, mp_n, counts, ids, places, gain_in, gain_ffn, voxels, w_qk, w_v, w_out, w_up,
    w_down, result,
    normed, index, column, digits, outbuf, nearbuf, arrived, spotbuf, spots, posb, padded,
    qk, vv, mixture, total, outans, ansz, ansx, voxp, resout, resx, acc, kept, out_all, up_all, down_all,
    zs, zr, ps, pr, ss, sr, az, ar, bs, br, cs, cr, ws, wr, fs, fr, ls,
):
    owners = spaces * subs
    far = owners - subs
    sp, sb, m = lax.axis_index("space"), lax.axis_index("sub"), lax.axis_index("mp")
    me = sp * subs + sb
    cap, part = outbuf.shape[1], outbuf.shape[2]
    rows, width = normed.shape
    piece = cap // mp_n
    ready = greet(owners, subs, mp_n, me, m)

    local = [
        pltpu.make_async_copy(w_qk, qk, ls.at[0]),
        pltpu.make_async_copy(w_v, vv, ls.at[1]),
        pltpu.make_async_copy(w_out, out_all.at[m], ls.at[2]),
        pltpu.make_async_copy(w_up, up_all.at[m], ls.at[3]),
        pltpu.make_async_copy(w_down, down_all.at[m], ls.at[4]),
    ]
    for c in local:
        c.start()

    def share(ref, full, lo, hi):
        n = ref.shape[0] // subs // 2
        return [(ref, full, n * 2, lo * n, (hi - lo) * n)]

    first = share(w_out, out_all, 0, 2) + share(w_up, up_all, 0, 1)
    second = share(w_up, up_all, 1, 2) + share(w_down, down_all, 0, 2)

    def weight_copy(k, entry, p, h):
        ref, full, stride, lo, n = entry
        here = pl.ds(pl.multiple_of(sb * stride + lo, 16), n)
        return remote(
            ref.at[here], full.at[h, here], (ws, wr), k * mp_n + p, {"mp": (m + p) % mp_n}
        )

    def weight_pass(k, entry, p, u, h, owner_sb):
        _, full, stride, lo, n = entry
        here = pl.ds(pl.multiple_of(owner_sb * stride + lo, 16), n)
        return remote(
            full.at[h, here], full.at[h, here], (fs, fr), (k * mp_n + p) * subs + u,
            {"sub": (sb + u) % subs},
        )

    def weights_send(entries, base):
        for k, entry in enumerate(entries):
            for p in range(1, mp_n):
                weight_copy(base + k, entry, p, m).start()

    def weights_forward(entries, base):
        for k, entry in enumerate(entries):
            for p in range(1, mp_n):
                h = (m + mp_n - p) % mp_n
                weight_copy(base + k, entry, p, h).wait()
                for u in range(1, subs):
                    weight_pass(base + k, entry, p, u, h, sb).start()

    def weights_done(entries, base):
        for k, entry in enumerate(entries):
            for p in range(1, mp_n):
                h = (m + mp_n - p) % mp_n
                for u in range(1, subs):
                    weight_pass(base + k, entry, p, u, h, (sb + subs - u) % subs).wait()

    span = math.gcd(rows, 256)
    olanes = max(owners, 8)
    before_mask = one_hot(iota((span, span), 0) < iota((span, span), 1))
    carry = jnp.zeros((olanes, 1), f32)
    for c in range(rows // span):
        here = slice(c * span, (c + 1) * span)
        window = ids[:, here]
        destination = lax.shift_right_logical(window, WIN_DEV.bit_length() - 1)
        position = (window - destination * WIN_DEV) * WLEN + places[:, here]
        target = jnp.where(destination == iota((olanes, span), 0), f32(1), f32(0))
        before = dot(target.astype(bf16), before_mask) + carry
        carry = carry + jnp.sum(target, axis=1, keepdims=True)
        rank = jnp.sum(before * target, axis=0, keepdims=True).astype(jnp.int32)
        index[:, here] = destination * cap + rank
        high = lax.shift_right_logical(position, BASE.bit_length() - 1)
        row = iota((8, span), 0)
        digits[:, here] = jnp.where(
            row == 0, high, jnp.where(row == 1, position - high * BASE, jnp.where(row == 2, 1, 0))
        ).astype(f32).astype(bf16)

    lump = math.gcd(rows, 256)

    def norm_step(b, carry):
        here = pl.ds(pl.multiple_of(b * lump, lump), lump)
        normed[here, :] = normalize(voxels[here, :].astype(f32), gain_in[...]).astype(bf16)
        return carry

    lax.fori_loop(0, rows // lump, norm_step, 0)

    def sink(slot):
        return (sp + slot // subs + 1) % spaces * subs + (sb + slot % subs) % subs

    def source(slot):
        return (sp + spaces - slot // subs - 1) % spaces * subs + (sb + subs - slot % subs) % subs

    def owner_id(t):
        return {"space": t // subs, "sub": t % subs}

    def find(slot, t):
        hit = one_hot(index[...] == iota((cap, rows), 0) + t * cap)
        parts = dot(digits[...], hit, ((1,), (1,)))
        place = parts[0:1] * BASE + parts[1:2] + (1 - parts[2:3]) * SLOTS
        spotbuf[slot] = place.astype(jnp.int32)
        return hit

    def spot_copy(slot, s, t):
        return remote(spotbuf.at[slot], spots.at[s], (ps, pr), slot, owner_id(t))

    def far_copy(slot, s, t):
        return remote(outbuf.at[slot], arrived.at[s, m], (zs, zr), slot, owner_id(t))

    def near_copy(j, s, t):
        return remote(nearbuf.at[j], arrived.at[s], (zs, zr), far + j, owner_id(t))

    def side_copy(slot, p, half, s):
        return remote(
            arrived.at[s, m], arrived.at[s, half], (ss, sr), slot * mp_n + p,
            {"mp": (m + p) % mp_n},
        )

    def send(slot):
        far_copy(slot, me, sink(slot)).start()
        spot_copy(slot, me, sink(slot)).start()

    ready()

    def build(slot, carry):
        hit = find(slot, sink(slot))
        mine = normed[:, pl.ds(pl.multiple_of(m * part, part), part)]
        outbuf[slot] = dot(hit, mine).astype(bf16)

        @pl.when(slot > 0)
        def _():
            send(slot - 1)

        return carry

    lax.fori_loop(0, far, build, 0)
    weights_send(first, 0)
    for j in range(subs):
        hit = find(far + j, sp * subs + (sb + j) % subs)
        for h in range(mp_n):
            nearbuf[j, h] = dot(hit, normed[:, h * part : (h + 1) * part]).astype(bf16)
        if j == 0:
            send(far - 1)
        elif j > 1:
            near_copy(j - 1, me, sp * subs + (sb + j - 1) % subs).start()
            spot_copy(far + j - 1, me, sp * subs + (sb + j - 1) % subs).start()
    spots[me] = spotbuf[far]
    posb[me] = column_of(spotbuf[far])
    chunk = 4 * WLEN

    def put(s, blocks, first):
        row = spots[s]

        def step(c, carry):
            start = pl.multiple_of(c * chunk, chunk)
            hit = one_hot(row == iota((chunk, cap), 0) + start)
            here = pl.ds(start, chunk)
            for h in range(mp_n):
                new = dot(hit, blocks[h]).astype(bf16)
                if not first:
                    new += padded[here, h * part : (h + 1) * part]
                padded[here, h * part : (h + 1) * part] = new
            return carry

        lax.fori_loop(0, padded.shape[0] // chunk, step, 0)

    def pick_voxels(slot):
        s = sink(slot)
        hit = one_hot(index[...] == iota((piece, rows), 0) + (s * cap + m * piece))
        voxp[s] = dot(hit, voxels[...]).astype(bf16)

    put(me, nearbuf.at[0], True)
    for j in range(max(subs - 1, 1), subs):
        near_copy(j, me, sp * subs + (sb + j) % subs).start()
        spot_copy(far + j, me, sp * subs + (sb + j) % subs).start()
    column[...] = column_of(index[...])
    for j in range(subs):
        pick_voxels(far + j)

    def settle(slot):
        s = source(slot)
        for p in range(1, mp_n):
            side_copy(slot, p, (m + mp_n - p) % mp_n, s).wait()
        spot_copy(slot, s, s).wait()
        posb[s] = column_of(spots[s])
        put(s, arrived.at[s], False)

    def onward(slot, carry):
        s = source(slot)
        far_copy(slot, s, s).wait()
        for p in range(1, mp_n):
            side_copy(slot, p, m, s).start()

        @pl.when(slot > 0)
        def _():
            settle(slot - 1)

        pick_voxels(slot)
        return carry

    lax.fori_loop(0, far, onward, 0)
    weights_send(second, len(first))
    for j in range(1, subs):
        s = sp * subs + (sb + subs - j) % subs
        near_copy(j, s, s).wait()
        spot_copy(far + j, s, s).wait()
        posb[s] = column_of(spots[s])
        put(s, arrived.at[s], False)
    weights_forward(first, 0)
    settle(far - 1)
    for c in local:
        c.wait()

    group = 2
    heads = part // HDIM
    head_of = iota((1, part), 1) // HDIM
    masks = [one_hot(head_of == h) for h in range(heads)]

    def attend(step, carry):
        start = pl.multiple_of(step * group * WLEN, group * WLEN)
        here = pl.ds(start, group * WLEN)
        rows_in = padded[here, :]
        queries = dot(rows_in, qk[0]).astype(bf16)
        keys = dot(rows_in, qk[1]).astype(bf16)
        values = dot(rows_in, vv[...]).astype(bf16)
        for g in range(group):
            inner = slice(g * WLEN, (g + 1) * WLEN)
            q, k, v = queries[inner], keys[inner], values[inner]
            stacked = jnp.concatenate([q * masks[h] for h in range(heads)], axis=0)
            scores = dot(stacked, k, ((1,), (1,))) * f32(HDIM ** -0.5)
            live = iota((1, WLEN), 1) < counts[me * WIN_DEV + step * group + g]
            scores = jnp.where(live, scores, f32(-1e30))
            weights = jnp.exp(scores - jnp.max(scores, axis=-1, keepdims=True))
            scale = 1.0 / jnp.sum(weights, axis=-1, keepdims=True)
            mixed = dot((weights * scale).astype(bf16), v)
            out = mixed[:WLEN]
            for h in range(1, heads):
                out = jnp.where(head_of == h, mixed[h * WLEN : (h + 1) * WLEN], out)
            mixture[pl.ds(start + g * WLEN, WLEN), :] = out.astype(bf16)
        return carry

    lax.fori_loop(0, WIN_DEV // group, attend, 0)

    def answer_copy(slot, s, t):
        return remote(outans.at[slot], ansz.at[s], (az, ar), slot, owner_id(t))

    def gather(t):
        place = posb[t]
        total[...] = jnp.zeros_like(total)

        def add(c, inner):
            start = pl.multiple_of(c * chunk, chunk)
            hit = one_hot(widen(place, chunk) == iota((cap, chunk), 1) + start)
            total[...] += dot(hit, mixture[pl.ds(start, chunk), :])
            return inner

        lax.fori_loop(0, SLOTS // chunk, add, 0)

    def reply(slot, carry):
        gather(sink(slot))
        for h in range(mp_n):
            outans[slot, h] = total[h * piece : (h + 1) * piece, :].astype(bf16)

        @pl.when((slot > 0) & (slot != far + 1))
        def _():
            answer_copy(slot - 1, me, sink(slot - 1)).start()

        return carry

    lax.fori_loop(0, owners, reply, 0)
    if subs > 1:
        answer_copy(owners - 1, me, sink(owners - 1)).start()
    ansz[me] = outans[far]
    acc[...] = jnp.zeros_like(acc)
    weights_forward(second, len(first))
    weights_done(first, 0)
    weights_done(second, len(first))

    def slot_of(i):
        return (i + far) % owners

    def swap_copy(i, p, s, src_m):
        return remote(
            ansz.at[s, (m + p) % mp_n], ansx.at[src_m, s], (bs, br), i * mp_n + p,
            {"mp": (m + p) % mp_n},
        )

    def give_copy(i, p, s, src_m):
        return remote(
            resout.at[s, (m + p) % mp_n], resx.at[s, src_m], (cs, cr), i * mp_n + p,
            {"mp": (m + p) % mp_n},
        )

    def finish(i, carry):
        @pl.when(i < owners)
        def _():
            slot = slot_of(i)
            s = source(slot)

            @pl.when(i > 0)
            def _():
                answer_copy(slot, s, s).wait()

            for p in range(1, mp_n):
                swap_copy(i, p, s, m).start()
            ansx[m, s] = ansz[s, m]

        @pl.when((i > 0) & (i <= owners))
        def _():
            s = source(slot_of(i - 1))
            for p in range(1, mp_n):
                swap_copy(i - 1, p, s, (m + mp_n - p) % mp_n).wait()
            after = voxp[s].astype(f32)
            for h in range(mp_n):
                after += dot(ansx[h, s], out_all[h])
            ready_rows = normalize(after, gain_ffn[...]).astype(bf16)
            kept[...] = after
            terms = None
            for h in range(mp_n):
                hidden = jax.nn.gelu(dot(ready_rows, up_all[h]), approximate=True).astype(bf16)
                part_sum = dot(hidden, down_all[h])
                terms = part_sum if terms is None else terms + part_sum
            done = (kept[...] + terms).astype(bf16)
            for h in range(mp_n):
                resout[s, h] = done[:, h * part : (h + 1) * part]

        @pl.when(i > 1)
        def _():
            s = source(slot_of(i - 2))
            for p in range(1, mp_n):
                give_copy(i - 2, p, s, (m + mp_n - p) % mp_n).wait()
            hit = one_hot(widen(column[...], cap) == iota((rows, cap), 1) + s * cap)
            acc[...] += dot(hit, resx[s].reshape(cap, part))

        @pl.when((i > 0) & (i <= owners))
        def _():
            s = source(slot_of(i - 1))
            for p in range(1, mp_n):
                give_copy(i - 1, p, s, m).start()
            resx[s, m] = resout[s, m]

        return carry

    lax.fori_loop(0, owners + 2, finish, 0)
    result[...] = acc[...].astype(bf16)


def shards(
    subs,
    voxels,
    window_ids,
    voxel_slots,
    window_counts,
    norm_gain,
    w_query_key,
    w_value,
    w_out,
    ffn_gain,
    w_up,
    w_down,
):
    owners = lax.axis_size(("space", "sub"))
    mp_n = lax.axis_size("mp")
    rows, width = voxels.shape
    part = width // mp_n
    unit = math.lcm(128, 16 * mp_n)
    cap = -(-(2 * rows // owners) // unit) * unit
    piece = cap // mp_n
    far = owners - subs
    dma = pltpu.SemaphoreType.DMA
    i32 = jnp.int32
    pieces = 4 * mp_n
    return pl.pallas_call(
        functools.partial(block_kernel, owners // subs, subs, mp_n),
        out_shape=jax.ShapeDtypeStruct((rows, part), bf16),
        in_specs=[SMEM] + [VMEM] * 5 + [ANY] * 5,
        out_specs=VMEM,
        scratch_shapes=[
            pltpu.VMEM((rows, width), bf16),
            pltpu.VMEM((1, rows), i32),
            pltpu.VMEM((rows, 128), i32),
            pltpu.VMEM((8, rows), bf16),
            pltpu.VMEM((far, cap, part), bf16),
            pltpu.VMEM((subs, mp_n, cap, part), bf16),
            pltpu.VMEM((owners, mp_n, cap, part), bf16),
            pltpu.VMEM((owners, 1, cap), i32),
            pltpu.VMEM((owners, 1, cap), i32),
            pltpu.VMEM((owners, cap, 128), i32),
            pltpu.VMEM((SLOTS, width), bf16),
            pltpu.VMEM(w_query_key.shape, bf16),
            pltpu.VMEM(w_value.shape, bf16),
            pltpu.VMEM((SLOTS, part), bf16),
            pltpu.VMEM((cap, part), f32),
            pltpu.VMEM((owners, mp_n, piece, part), bf16),
            pltpu.VMEM((owners, mp_n, piece, part), bf16),
            pltpu.VMEM((mp_n, owners, piece, part), bf16),
            pltpu.VMEM((owners, piece, width), bf16),
            pltpu.VMEM((owners, mp_n, piece, part), bf16),
            pltpu.VMEM((owners, mp_n, piece, part), bf16),
            pltpu.VMEM((rows, part), f32),
            pltpu.VMEM((piece, width), f32),
            pltpu.VMEM((mp_n,) + w_out.shape, bf16),
            pltpu.VMEM((mp_n,) + w_up.shape, bf16),
            pltpu.VMEM((mp_n,) + w_down.shape, bf16),
            dma((owners,)), dma((owners,)), dma((owners,)), dma((owners,)),
            dma((far * mp_n,)), dma((far * mp_n,)),
            dma((owners,)), dma((owners,)),
            dma((owners * mp_n,)), dma((owners * mp_n,)),
            dma((owners * mp_n,)), dma((owners * mp_n,)),
            dma((pieces,)), dma((pieces,)),
            dma((pieces * subs,)), dma((pieces * subs,)),
            dma((5,)),
        ],
        compiler_params=pltpu.CompilerParams(
            collective_id=0, has_side_effects=True, vmem_limit_bytes=62 * 1024 * 1024
        ),
        name="block",
    )(
        window_counts, window_ids[None, :], voxel_slots[None, :], norm_gain[None, :],
        ffn_gain[None, :], voxels, w_query_key, w_value, w_out, w_up, w_down,
    )


def solution(mesh):
    return jax.shard_map(
        functools.partial(shards, mesh.shape["sub"]),
        mesh=mesh,
        in_specs=(
            P(("groups", "space", "sub"), None),
            P(("groups", "space", "sub")),
            P(("groups", "space", "sub")),
            P("groups"),
            P(),
            P(None, None, "mp"),
            P(None, "mp"),
            P("mp", None),
            P(),
            P(None, "mp"),
            P("mp", None),
        ),
        out_specs=P(("groups", "space", "sub"), "mp"),
        check_vma=False,
    )
```

time: 184 us -> 142 us (0.77)
  Pallas kernels: 168 us -> 137 us
  other arithmetic: 8.4 us -> 0 us
  local copies, waits for them, and re-layouts: 6.86 us -> 4.65 us
    pallas_call x4 -> x1, Pallas kernels: 168 us -> 137 us  [shards(): pl.pallas_call(functools.partial(block_kernel, owners // subs, subs, mp_n...]
    another operation x4 -> x0, other arithmetic: 3.31 us -> none
    reduce_sum x3 -> x0, other arithmetic: 2.58 us -> none  [the longest x1 1.69 us: normalize(): row_mean = jnp.mean(values_in, axis=-1, keepdims=True)]
where the time goes in v1:
time: 142 us; the launch traced here: 141 us
  Pallas kernels  137 us (96%)
  local copies, waits for them, and re-layouts  4.65 us (3%)
    pallas_call x1, Pallas kernels, shards(): pl.pallas_call(functools.partial(block_kernel, owners // subs, subs, mp_n...  137 us

profile of v1, /device:TPU:12, one launch (start us, length us, event | category | flops | bytes accessed | tf_op | source)
XLA Modules:
  0.0 141.5 jit_solution(854917300807050838)
XLA Ops:
  0.0 1.3 broadcast_in_dim.12.ids
  1.3 1.3 broadcast_in_dim.13.places
  2.6 136.8 %block.1 = bf16[1536,256]{1,0:T(8,128)(2,1)} custom-call(s32[128]{0:T(128)} %counts.1, s32[1,1536]{1,0:T(1,128)} %broadcast_in_dim.12.ids, s32[1,1536]{1,0:T(1,128)} %broadcast_in_dim.13.places, f32[1,512]{1,0:T(1,128)} %bitcast.2, f32[1,512]{1,0:T(1,128)} %bitcast.3, bf16[1536,512]{1,0:T(8,128)(2,1)} %voxels.1, bf16[2,512,256]{2,1,0:T(8,128)(2,1)} %w_qk.1, ...), custom_call_target="tpu_custom_call" | custom-call | tf_op jit(solution)/shard_map/block/pallas_call | solution.py:458
  139.4 2.1 %copy.13 = bf16[1536,256]{1,0:T(8,128)(2,1)} copy(bf16[1536,256]{1,0:T(8,128)(2,1)} %block.1) | data formatting | bytes 1572864

commit v2 on v1

v2 whole, which is shorter than its diff:
```python
import functools
import math

import jax
import jax.numpy as jnp
from jax import lax
from jax.experimental import pallas as pl
from jax.experimental.pallas import tpu as pltpu
from jax.sharding import PartitionSpec as P

HDIM = 64
WLEN = 256
WIN_DEV = 16
BASE = 64
SLOTS = WIN_DEV * WLEN
MESH = pl.DeviceIdType.MESH
VMEM = pl.BlockSpec(memory_space=pltpu.VMEM)
SMEM = pl.BlockSpec(memory_space=pltpu.SMEM)
ANY = pl.BlockSpec(memory_space=pl.ANY)
f32 = jnp.float32
bf16 = jnp.bfloat16


def normalize(values_in, gain):
    row_mean = jnp.mean(values_in, axis=-1, keepdims=True)
    centred = values_in - row_mean
    variance = jnp.mean(centred * centred, axis=-1, keepdims=True)
    return centred * lax.rsqrt(variance + 1e-05) * gain


def iota(shape, dim):
    return lax.broadcasted_iota(jnp.int32, shape, dim)


def one_hot(found):
    return jnp.where(found, f32(1), f32(0)).astype(bf16)


def dot(a, b, dims=((1,), (0,))):
    return lax.dot_general(a, b, (dims, ((), ())), preferred_element_type=f32)


def greet(groups, spaces, subs, mp_n, g, sp, sb, m):
    barrier = pltpu.get_barrier_semaphore()
    everyone = spaces * subs * mp_n
    me = (sp * subs + sb) * mp_n + m
    for k in range(1, everyone):
        t = (me + k) % everyone
        pl.semaphore_signal(
            barrier,
            inc=1,
            device_id={"space": t // mp_n // subs, "sub": t // mp_n % subs, "mp": t % mp_n},
            device_id_type=MESH,
        )
    for k in range(1, groups):
        for u in range(subs):
            pl.semaphore_signal(
                barrier, inc=1, device_id={"groups": (g + k) % groups, "sub": u},
                device_id_type=MESH,
            )
    return lambda: pl.semaphore_wait(barrier, everyone - 1 + (groups - 1) * subs)


def remote(src, dst, sems, index, device):
    return pltpu.make_async_remote_copy(
        src_ref=src,
        dst_ref=dst,
        send_sem=sems[0].at[index],
        recv_sem=sems[1].at[index],
        device_id=device,
        device_id_type=MESH,
    )


def column_of(row):
    return jnp.transpose(jnp.broadcast_to(row, (128, row.shape[1])))


def widen(column, width):
    return jnp.concatenate([column] * (width // 128), axis=1)


def block_kernel(
    groups, spaces, subs, mp_n, counts, places, gain_in, gain_ffn, voxels, w_qk, w_v, w_out, w_up,
    w_down, result,
    normed, index, column, digits, outbuf, nearbuf, arrived, spotbuf, spots, posb, padded,
    qk, vv, mixture, total, outans, ansx, voxp, resout, resx, acc, kept, out_all, up_all, down_all,
    zs, zr, ns, nr, ps, pr, ss, sr, az, ar, cs, cr, ws, wr, fs, fr, ls,
):
    owners = spaces * subs
    far = owners - subs
    sp, sb, m = lax.axis_index("space"), lax.axis_index("sub"), lax.axis_index("mp")
    me = sp * subs + sb
    cap, part = outbuf.shape[1], outbuf.shape[2]
    rows, width = normed.shape
    piece = cap // mp_n
    g = lax.axis_index("groups")
    ready = greet(groups, spaces, subs, mp_n, g, sp, sb, m)

    local = [
        pltpu.make_async_copy(w_qk, qk, ls.at[0]),
        pltpu.make_async_copy(w_v, vv, ls.at[1]),
        pltpu.make_async_copy(w_out, out_all.at[m], ls.at[2]),
        pltpu.make_async_copy(w_up, up_all.at[m], ls.at[3]),
        pltpu.make_async_copy(w_down, down_all.at[m], ls.at[4]),
    ]
    for c in local:
        c.start()

    shares = groups * subs
    tables = ((w_out, out_all), (w_up, up_all), (w_down, down_all))

    def share_rows(ref, dg, du):
        n = ref.shape[0] // shares
        e = (g + dg) % groups * subs + (sb + du) % subs
        return pl.ds(pl.multiple_of(e * n, n), n)

    def weight_copy(k, p, h):
        ref, full = tables[k]
        here = share_rows(ref, 0, 0)
        return remote(
            ref.at[here], full.at[h, here], (ws, wr), k * mp_n + p, {"mp": (m + p) % mp_n}
        )

    def weight_pass(k, p, dg, du, h, back):
        ref, full = tables[k]
        here = share_rows(ref, groups - dg, subs - du) if back else share_rows(ref, 0, 0)
        return remote(
            full.at[h, here], full.at[h, here], (fs, fr),
            ((k * mp_n + p) * groups + dg) * subs + du,
            {"groups": (g + dg) % groups, "sub": (sb + du) % subs},
        )

    others = [(dg, du) for dg in range(groups) for du in range(subs) if dg + du > 0]

    def weights_send(which):
        for k in which:
            for p in range(1, mp_n):
                weight_copy(k, p, m).start()

    def weights_forward(which):
        for k in which:
            for p in range(1, mp_n):
                h = (m + mp_n - p) % mp_n
                weight_copy(k, p, h).wait()
                for dg, du in others:
                    weight_pass(k, p, dg, du, h, False).start()

    def weights_done():
        for k in range(3):
            for p in range(1, mp_n):
                for dg, du in others:
                    weight_pass(k, p, dg, du, (m + mp_n - p) % mp_n, True).wait()

    span = math.gcd(rows, 256)
    olanes = max(owners, 8)
    before_mask = one_hot(iota((span, span), 0) < iota((span, span), 1))
    carry = jnp.zeros((olanes, 1), f32)
    for c in range(rows // span):
        here = slice(c * span, (c + 1) * span)
        place = places[:, here]
        destination = lax.shift_right_logical(place, SLOTS.bit_length() - 1)
        position = place - destination * SLOTS
        target = jnp.where(destination == iota((olanes, span), 0), f32(1), f32(0))
        before = dot(target.astype(bf16), before_mask) + carry
        carry = carry + jnp.sum(target, axis=1, keepdims=True)
        rank = jnp.sum(before * target, axis=0, keepdims=True).astype(jnp.int32)
        index[:, here] = destination * cap + rank
        high = lax.shift_right_logical(position, BASE.bit_length() - 1)
        row = iota((8, span), 0)
        digits[:, here] = jnp.where(
            row == 0, high, jnp.where(row == 1, position - high * BASE, jnp.where(row == 2, 1, 0))
        ).astype(f32).astype(bf16)

    lump = math.gcd(rows, 256)

    def norm_step(b, carry):
        here = pl.ds(pl.multiple_of(b * lump, lump), lump)
        normed[here, :] = normalize(voxels[here, :].astype(f32), gain_in[...]).astype(bf16)
        return carry

    lax.fori_loop(0, rows // lump, norm_step, 0)

    def sink(slot):
        return (sp + slot // subs + 1) % spaces * subs + (sb + slot % subs) % subs

    def source(slot):
        return (sp + spaces - slot // subs - 1) % spaces * subs + (sb + subs - slot % subs) % subs

    def owner_id(t):
        return {"space": t // subs, "sub": t % subs}

    def find(slot, t):
        hit = one_hot(index[...] == iota((cap, rows), 0) + t * cap)
        parts = dot(digits[...], hit, ((1,), (1,)))
        place = parts[0:1] * BASE + parts[1:2] + (1 - parts[2:3]) * SLOTS
        spotbuf[slot] = place.astype(jnp.int32)
        return hit

    def slot_of(i):
        return (i + far) % owners

    def spot_copy(slot, s, t):
        return remote(spotbuf.at[slot], spots.at[s], (ps, pr), slot, owner_id(t))

    def part_rows(q):
        return pl.ds(q * piece, piece)

    def far_copy(slot, q, s, t):
        return remote(
            outbuf.at[slot, part_rows(q)], arrived.at[s, m, part_rows(q)], (zs, zr),
            slot * mp_n + q, owner_id(t),
        )

    def near_copy(slot, s, t):
        return remote(nearbuf.at[slot - far], arrived.at[s], (ns, nr), slot - far, owner_id(t))

    def side_copy(slot, q, p, half, s):
        return remote(
            arrived.at[s, m, part_rows(q)], arrived.at[s, half, part_rows(q)], (ss, sr),
            (slot * mp_n + q) * mp_n + p, {"mp": (m + p) % mp_n},
        )

    ready()

    def build(slot, carry):
        t = sink(slot)
        hit = one_hot(index[...] == iota((cap, rows), 0) + t * cap)
        mine = normed[:, pl.ds(pl.multiple_of(m * part, part), part)]
        outbuf[slot] = dot(hit, mine).astype(bf16)
        for q in range(mp_n):
            far_copy(slot, q, me, t).start()
        return carry

    lax.fori_loop(0, far, build, 0)
    weights_send((0, 1))

    def near_build():
        for j in range(subs):
            t = sink(far + j)
            hit = find(far + j, t)
            for h in range(mp_n):
                packed = dot(hit, normed[:, h * part : (h + 1) * part]).astype(bf16)
                if j == 0:
                    arrived[me, h] = packed
                else:
                    nearbuf[j, h] = packed
            if j == 0:
                spots[me] = spotbuf[far]
            else:
                near_copy(far + j, me, t).start()
                spot_copy(far + j, me, t).start()

    chunk = 4 * WLEN

    def put(base, first):
        row = jnp.concatenate([spots[base + u] for u in range(subs)], axis=1)

        def step(c, carry):
            start = pl.multiple_of(c * chunk, chunk)
            hit = one_hot(row == iota((chunk, subs * cap), 0) + start)
            here = pl.ds(start, chunk)
            for h in range(mp_n):
                block = arrived[pl.ds(base, subs), h].reshape(subs * cap, part)
                new = dot(hit, block).astype(bf16)
                if not first:
                    new += padded[here, h * part : (h + 1) * part]
                padded[here, h * part : (h + 1) * part] = new
            return carry

        lax.fori_loop(0, padded.shape[0] // chunk, step, 0)

    def pick_voxels(slot):
        s = sink(slot)
        hit = one_hot(index[...] == iota((piece, rows), 0) + (s * cap + m * piece))
        voxp[s] = dot(hit, voxels[...]).astype(bf16)

    def settle_near():
        for u in range(1, subs):
            s = source(far + u)
            near_copy(far + u, s, s).wait()
            spot_copy(far + u, s, s).wait()
        for u in range(subs):
            posb[sp * subs + u] = column_of(spots[sp * subs + u])
        put(sp * subs, True)

    def settle(chip):
        base = source(chip * subs) // subs * subs
        for u in range(subs):
            slot = chip * subs + u
            s = source(slot)
            for q in range(mp_n):
                for p in range(1, mp_n):
                    side_copy(slot, q, p, (m + mp_n - p) % mp_n, s).wait()
            spot_copy(slot, s, s).wait()
            posb[s] = column_of(spots[s])
        put(base, False)

    def onward(slot, carry):
        s = source(slot)
        for q in range(mp_n):
            far_copy(slot, q, s, s).wait()
            for p in range(1, mp_n):
                side_copy(slot, q, p, m, s).start()
        @pl.when(slot == 0)
        def _():
            near_build()
            column[...] = column_of(index[...])

        t = sink(slot)
        find(slot, t)
        pick_voxels(slot)
        spot_copy(slot, me, t).start()

        @pl.when(slot == subs - 1)
        def _():
            settle_near()

        @pl.when((slot > subs - 1) & (slot % subs == subs - 1))
        def _():
            settle(slot // subs - 1)

        return carry

    lax.fori_loop(0, far, onward, 0)
    weights_forward((0, 1))
    weights_send((2,))
    for j in range(subs):
        pick_voxels(far + j)
    settle(spaces - 2)
    for c in local:
        c.wait()

    group = 2
    heads = part // HDIM
    head_of = iota((1, part), 1) // HDIM
    masks = [one_hot(head_of == h) for h in range(heads)]

    def attend(step, carry):
        @pl.when(step == WIN_DEV // group * 3 // 4)
        def _():
            weights_forward((2,))

        start = pl.multiple_of(step * group * WLEN, group * WLEN)
        here = pl.ds(start, group * WLEN)
        rows_in = padded[here, :]
        queries = dot(rows_in, qk[0]).astype(bf16) * bf16(HDIM ** -0.5)
        keys = dot(rows_in, qk[1]).astype(bf16)
        values = dot(rows_in, vv[...]).astype(bf16)
        for g in range(group):
            inner = slice(g * WLEN, (g + 1) * WLEN)
            q, k, v = queries[inner], keys[inner], values[inner]
            stacked = jnp.concatenate([q * masks[h] for h in range(heads)], axis=0)
            scores = dot(stacked, k, ((1,), (1,)))
            live = iota((1, WLEN), 1) < counts[me * WIN_DEV + step * group + g]
            scores = jnp.where(live, scores, f32(-1e30))
            weights = jnp.exp(scores - jnp.max(scores, axis=-1, keepdims=True))
            scale = 1.0 / jnp.sum(weights, axis=-1, keepdims=True)
            mixed = dot(weights.astype(bf16), v)
            out = mixed[:WLEN] * scale[:WLEN]
            for h in range(1, heads):
                rows_h = slice(h * WLEN, (h + 1) * WLEN)
                out = jnp.where(head_of == h, mixed[rows_h] * scale[rows_h], out)
            mixture[pl.ds(start + g * WLEN, WLEN), :] = out.astype(bf16)
        return carry

    lax.fori_loop(0, WIN_DEV // group, attend, 0)

    def answer_copy(slot, d, s, t, src_m):
        target = {**owner_id(t), "mp": (m + d) % mp_n}
        return remote(
            outans.at[slot, (m + d) % mp_n], ansx.at[src_m, s], (az, ar), slot * mp_n + d, target
        )

    def gather(t):
        place = posb[t]
        total[...] = jnp.zeros_like(total)

        def add(c, inner):
            start = pl.multiple_of(c * chunk, chunk)
            hit = one_hot(widen(place, chunk) == iota((cap, chunk), 1) + start)
            total[...] += dot(hit, mixture[pl.ds(start, chunk), :])
            return inner

        lax.fori_loop(0, SLOTS // chunk, add, 0)

    def reply(r, carry):
        slot = jnp.where(r < subs, r, jnp.where(r < 2 * subs, far + r - subs, r - subs))
        t = sink(slot)
        gather(t)
        for h in range(mp_n):
            outans[slot, h] = total[h * piece : (h + 1) * piece, :].astype(bf16)
        for d in range(1, mp_n):
            answer_copy(slot, d, me, t, m).start()

        @pl.when(slot != far)
        def _():
            answer_copy(slot, 0, me, t, m).start()

        return carry

    lax.fori_loop(0, owners, reply, 0)
    ansx[m, me] = outans[far, m]
    acc[...] = jnp.zeros_like(acc)
    weights_done()

    def give_copy(i, p, s, src_m):
        return remote(
            resout.at[s, (m + p) % mp_n], resx.at[s, src_m], (cs, cr), i * mp_n + p,
            {"mp": (m + p) % mp_n},
        )

    def finish(i, carry):
        @pl.when(i < owners)
        def _():
            slot = slot_of(i)
            s = source(slot)
            for d in range(1, mp_n):
                answer_copy(slot, d, s, s, (m + mp_n - d) % mp_n).wait()

            @pl.when(i > 0)
            def _():
                answer_copy(slot, 0, s, s, m).wait()

            after = voxp[s].astype(f32)
            for h in range(mp_n):
                after += dot(ansx[h, s], out_all[h])
            ready_rows = normalize(after, gain_ffn[...]).astype(bf16)
            kept[...] = after
            terms = None
            for h in range(mp_n):
                hidden = jax.nn.gelu(dot(ready_rows, up_all[h]), approximate=True).astype(bf16)
                part_sum = dot(hidden, down_all[h])
                terms = part_sum if terms is None else terms + part_sum
            done = (kept[...] + terms).astype(bf16)
            for h in range(mp_n):
                resout[s, h] = done[:, h * part : (h + 1) * part]

        @pl.when(i > 1)
        def _():
            s = source(slot_of(i - 2))
            for p in range(1, mp_n):
                give_copy(i - 2, p, s, (m + mp_n - p) % mp_n).wait()
            hit = one_hot(widen(column[...], cap) == iota((rows, cap), 1) + s * cap)
            acc[...] += dot(hit, resx[s].reshape(cap, part))

        @pl.when(i < owners)
        def _():
            s = source(slot_of(i))
            for p in range(1, mp_n):
                give_copy(i, p, s, m).start()
            resx[s, m] = resout[s, m]

        return carry

    lax.fori_loop(0, owners + 2, finish, 0)
    result[...] = acc[...].astype(bf16)


def shards(
    subs,
    voxels,
    window_ids,
    voxel_slots,
    window_counts,
    norm_gain,
    w_query_key,
    w_value,
    w_out,
    ffn_gain,
    w_up,
    w_down,
):
    groups = lax.axis_size("groups")
    owners = lax.axis_size(("space", "sub"))
    mp_n = lax.axis_size("mp")
    rows, width = voxels.shape
    part = width // mp_n
    unit = math.lcm(128, 16 * mp_n)
    cap = -(-(2 * rows // owners) // unit) * unit
    piece = cap // mp_n
    far = owners - subs
    dma = pltpu.SemaphoreType.DMA
    i32 = jnp.int32
    pieces = 3 * mp_n
    return pl.pallas_call(
        functools.partial(block_kernel, groups, owners // subs, subs, mp_n),
        out_shape=jax.ShapeDtypeStruct((rows, part), bf16),
        in_specs=[SMEM] + [VMEM] * 4 + [ANY] * 5,
        out_specs=VMEM,
        scratch_shapes=[
            pltpu.VMEM((rows, width), bf16),
            pltpu.VMEM((1, rows), i32),
            pltpu.VMEM((rows, 128), i32),
            pltpu.VMEM((8, rows), bf16),
            pltpu.VMEM((far, cap, part), bf16),
            pltpu.VMEM((subs, mp_n, cap, part), bf16),
            pltpu.VMEM((owners, mp_n, cap, part), bf16),
            pltpu.VMEM((owners, 1, cap), i32),
            pltpu.VMEM((owners, 1, cap), i32),
            pltpu.VMEM((owners, cap, 128), i32),
            pltpu.VMEM((SLOTS, width), bf16),
            pltpu.VMEM(w_query_key.shape, bf16),
            pltpu.VMEM(w_value.shape, bf16),
            pltpu.VMEM((SLOTS, part), bf16),
            pltpu.VMEM((cap, part), f32),
            pltpu.VMEM((owners, mp_n, piece, part), bf16),
            pltpu.VMEM((mp_n, owners, piece, part), bf16),
            pltpu.VMEM((owners, piece, width), bf16),
            pltpu.VMEM((owners, mp_n, piece, part), bf16),
            pltpu.VMEM((owners, mp_n, piece, part), bf16),
            pltpu.VMEM((rows, part), f32),
            pltpu.VMEM((piece, width), f32),
            pltpu.VMEM((mp_n,) + w_out.shape, bf16),
            pltpu.VMEM((mp_n,) + w_up.shape, bf16),
            pltpu.VMEM((mp_n,) + w_down.shape, bf16),
            dma((far * mp_n,)), dma((far * mp_n,)), dma((subs,)), dma((subs,)),
            dma((owners,)), dma((owners,)),
            dma((far * mp_n * mp_n,)), dma((far * mp_n * mp_n,)),
            dma((owners * mp_n,)), dma((owners * mp_n,)),
            dma((owners * mp_n,)), dma((owners * mp_n,)),
            dma((pieces,)), dma((pieces,)),
            dma((pieces * groups * subs,)), dma((pieces * groups * subs,)),
            dma((5,)),
        ],
        compiler_params=pltpu.CompilerParams(
            collective_id=0, has_side_effects=True, vmem_limit_bytes=62 * 1024 * 1024
        ),
        name="block",
    )(
        window_counts, (window_ids * WLEN + voxel_slots)[None, :], norm_gain[None, :],
        ffn_gain[None, :], voxels, w_query_key, w_value, w_out, w_up, w_down,
    )


def solution(mesh):
    return jax.shard_map(
        functools.partial(shards, mesh.shape["sub"]),
        mesh=mesh,
        in_specs=(
            P(("groups", "space", "sub"), None),
            P(("groups", "space", "sub")),
            P(("groups", "space", "sub")),
            P("groups"),
            P(),
            P(None, None, "mp"),
            P(None, "mp"),
            P("mp", None),
            P(),
            P(None, "mp"),
            P("mp", None),
        ),
        out_specs=P(("groups", "space", "sub"), "mp"),
        check_vma=False,
    )
```

time: 142 us -> 124 us (0.87)
  Pallas kernels: 137 us -> 121 us
  local copies, waits for them, and re-layouts: 4.65 us -> 2.66 us
    pallas_call x1, Pallas kernels: 137 us -> 121 us  [shards(): pl.pallas_call(functools.partial(block_kernel, groups, owners // subs, su...]
    broadcast_in_dim x2 -> x1, local copies, waits for them, and re-layouts: 2.58 us -> 0.6 us  [shards(): (window_ids * WLEN + voxel_slots)[None, :]]
where the time goes in v2:
time: 124 us
  Pallas kernels  121 us (98%)
  local copies, waits for them, and re-layouts  2.66 us (2%)
    pallas_call x1, Pallas kernels, shards(): pl.pallas_call(functools.partial(block_kernel, groups, owners // subs, su...  121 us

profile of v2, /device:TPU:12, one launch (start us, length us, event | category | flops | bytes accessed | tf_op | source)
XLA Modules:
  0.0 124.0 jit_solution(13867969136770814598)
XLA Ops:
  0.0 0.7 multiply_add_fusion
  0.7 0.6 broadcast_in_dim.9.places
  1.3 120.6 %block.1 = bf16[1536,256]{1,0:T(8,128)(2,1)} custom-call(s32[128]{0:T(128)} %counts.1, s32[1,1536]{1,0:T(1,128)} %broadcast_in_dim.9.places, f32[1,512]{1,0:T(1,128)} %bitcast.2, f32[1,512]{1,0:T(1,128)} %bitcast.3, bf16[1536,512]{1,0:T(8,128)(2,1)} %voxels.1, bf16[2,512,256]{2,1,0:T(8,128)(2,1)} %w_qk.1, bf16[512,256]{1,0:T(8,128)(2,1)} %w_v.1, ...), custom_call_target="tpu_custom_call" | custom-call | tf_op jit(solution)/shard_map/block/pallas_call | solution.py:486
  122.0 2.1 %copy.13 = bf16[1536,256]{1,0:T(8,128)(2,1)} copy(bf16[1536,256]{1,0:T(8,128)(2,1)} %block.1) | data formatting | bytes 1572864

commit v3 on v2

--- a/solution.py
+++ b/solution.py
@@ -158,7 +158,9 @@
     carry = jnp.zeros((olanes, 1), f32)
     for c in range(rows // span):
         here = slice(c * span, (c + 1) * span)
-        place = places[:, here]
+        place = jnp.concatenate(
+            [places[r : r + 1, :] for r in range(here.start // 128, here.stop // 128)], axis=1
+        )
         destination = lax.shift_right_logical(place, SLOTS.bit_length() - 1)
         position = place - destination * SLOTS
         target = jnp.where(destination == iota((olanes, span), 0), f32(1), f32(0))
@@ -331,7 +333,7 @@
     for c in local:
         c.wait()
 
-    group = 2
+    group = 4
     heads = part // HDIM
     head_of = iota((1, part), 1) // HDIM
     masks = [one_hot(head_of == h) for h in range(heads)]
@@ -528,7 +530,7 @@
         ),
         name="block",
     )(
-        window_counts, (window_ids * WLEN + voxel_slots)[None, :], norm_gain[None, :],
+        window_counts, (window_ids * WLEN + voxel_slots).reshape(rows // 128, 128), norm_gain[None, :],
         ffn_gain[None, :], voxels, w_query_key, w_value, w_out, w_up, w_down,
     )
 

time: 124 us -> 123 us (level)
  Pallas kernels: 121 us -> 119 us
    pallas_call x1, Pallas kernels: 121 us -> 119 us  [shards(): pl.pallas_call(functools.partial(block_kernel, groups, owners // subs, su...]
    reshape x0 -> x1, other arithmetic: none -> 1.31 us  [shards(): (window_ids * WLEN + voxel_slots).reshape(rows // 128, 128)]
where the time goes in v3:
time: 123 us; the launch traced here: 122 us
  Pallas kernels  119 us (97%)
  local copies, waits for them, and re-layouts  2.06 us (2%)
  other arithmetic  1.31 us (1%)
    pallas_call x1, Pallas kernels, shards(): pl.pallas_call(functools.partial(block_kernel, groups, owners // subs, su...  119 us

profile of v3, /device:TPU:12, one launch (start us, length us, event | category | flops | bytes accessed | tf_op | source)
XLA Modules:
  0.0 122.3 jit_solution(6101878061417540422)
XLA Ops:
  0.0 1.3 %add_bitcast_fusion.places = s32[12,128]{1,0:T(8,128)} fusion(s32[1536]{0:T(1024)} %param.13, s32[1536]{0:T(1024)} %param.12), kind=kLoop, calls=%fused_computation | loop fusion | flops 3072 | bytes 18432 | tf_op jit(solution)/shard_map/reshape | solution.py:533
  1.3 119.0 %block.1 = bf16[1536,256]{1,0:T(8,128)(2,1)} custom-call(s32[128]{0:T(128)} %counts.1, s32[12,128]{1,0:T(8,128)} %add_bitcast_fusion.places, f32[1,512]{1,0:T(1,128)} %bitcast.4, f32[1,512]{1,0:T(1,128)} %bitcast.5, bf16[1536,512]{1,0:T(8,128)(2,1)} %voxels.1, bf16[2,512,256]{2,1,0:T(8,128)(2,1)} %w_qk.1, bf16[512,256]{1,0:T(8,128)(2,1)} %w_v.1, ...), custom_call_target="tpu_custom_call" | custom-call | tf_op jit(solution)/shard_map/block/pallas_call | solution.py:488
  120.3 2.1 %copy.13 = bf16[1536,256]{1,0:T(8,128)(2,1)} copy(bf16[1536,256]{1,0:T(8,128)(2,1)} %block.1) | data formatting | bytes 1572864
